TPU v7x, 32 devices: a whole 2x2x4 slice. The times are simulated.
32 devices in a mesh: seq: 16 (over z, y, core), mp: 2 (over x).
Axes of the slice: x: 2, y: 2, z: 4, core: 2. Of those that a mesh axis runs over, the one named last changes fastest.
Arguments:
- query: bfloat16 [4096, 3072], P('seq', 'mp'), may hold values from -4.5 to 4.5
- key: bfloat16 [4096, 3072], P('seq', 'mp'), may hold values from -4.5 to 4.5
- value: bfloat16 [4096, 3072], P('seq', 'mp'), may hold values from -6 to 6
- clip_lengths: int32 [4, 4], replicated, may hold values from 0 to 1024, as said below
Outputs:
- attended: bfloat16 [4096, 3072], P(('seq', 'mp'))
Inputs may be any that keep to these rules, and one draw needn't show every extreme that they name: `clip_lengths`: each row sums to 1024; a clip slot may be empty; in some bucket one clip fills all 1024 tokens.
All inputs are finite; a program needn't handle non-finite values.
Results may differ from a plain program's by a relative error of at most 0.01.
Values may be sent and summed in bfloat16 or wider, within the bound.
A program may use at most 64 MiB of HBM per device.

v0:
```python
import jax
import jax.numpy as jnp
from jax import lax
from jax.sharding import PartitionSpec as P

HD = 128


NEG = -1e30


def from_partner(array, axis, apart):
    return lax.ppermute(array, axis, [(i, i ^ 1 << apart) for i in range(lax.axis_size(axis))])


def shards(query, key, value, clip_lengths):
    tok_rows = query.shape[0]
    width = query.shape[1]
    heads = width // HD
    scale = 1.0 / HD**0.5
    group = lax.axis_size("seq") // 4
    levels = group.bit_length() - 1
    span = tok_rows * group
    buckets = clip_lengths.shape[0]
    slots = clip_lengths.shape[1]
    me_index = lax.axis_index("seq")
    start = me_index * tok_rows
    home_bucket = me_index // group
    ends = jnp.cumsum(clip_lengths, axis=1)
    bucket_ids = jnp.arange(buckets, dtype=jnp.int32)

    def clip_of(places):
        bucket = places // span
        offset = places - bucket * span
        hits = jnp.sum((offset[:, None, None] >= ends[None, :, :]).astype(jnp.int32), axis=2)
        pick = bucket[:, None] == bucket_ids[None, :]
        inner = jnp.sum(jnp.where(pick, hits, 0), axis=1)
        return bucket * slots + inner

    limit = home_bucket * span + span
    q_ids = clip_of(start + jnp.arange(tok_rows, dtype=jnp.int32))
    queries = query.reshape(tok_rows, heads, HD)

    def attend(carry, q_rows, q_clip, key_block, value_block, first, bound):
        count = key_block.shape[0]
        keys = key_block.reshape(count, heads, HD)
        values = value_block.reshape(count, heads, HD)
        k_ids = clip_of(first + jnp.arange(count, dtype=jnp.int32))

        def update(state):
            top_old, total_old, summed_old = state
            score = (
                jnp.einsum("qhd,khd->hqk", q_rows, keys, preferred_element_type=jnp.float32) * scale
            )
            keep = (q_clip[:, None] == k_ids[None, :])[None]
            score = jnp.where(keep, score, NEG)
            top_new = jnp.maximum(top_old, jnp.max(score, axis=-1))
            weight = jnp.where(keep, jnp.exp(score - top_new[:, :, None]), 0.0)
            factor = jnp.exp(top_old - top_new)
            total_new = total_old * factor + jnp.sum(weight, axis=-1)
            added = jnp.einsum(
                "hqk,khd->qhd",
                weight.astype(jnp.bfloat16),
                values,
                preferred_element_type=jnp.float32,
            )
            summed_new = summed_old * jnp.transpose(factor)[:, :, None] + added
            return (top_new, total_new, summed_new)

        needed = first < bound
        needed = needed & jnp.any((k_ids >= q_clip[0]) & (k_ids <= q_clip[-1]))
        return lax.cond(needed, update, lambda state: state, carry)

    initial = (
        jnp.full((heads, tok_rows), NEG, jnp.float32),
        jnp.zeros((heads, tok_rows), jnp.float32),
        jnp.zeros((tok_rows, heads, HD), jnp.float32),
    )
    held = (key, value)
    pieces = [(held, start)]
    for bit in range(levels):
        received = from_partner((held[0], held[1]), "seq", bit)
        stride = 2**bit
        own_base = me_index // stride * stride
        partner_upper = me_index // stride % 2
        pieces.append((received, (own_base + stride - 2 * stride * partner_upper) * tok_rows))
        if bit + 1 < levels:
            upper = me_index // 2**bit % 2 == 1
            lower_keys = jnp.where(upper, received[0], held[0])
            higher_keys = jnp.where(upper, held[0], received[0])
            lower_values = jnp.where(upper, received[1], held[1])
            higher_values = jnp.where(upper, held[1], received[1])
            held = (
                jnp.concatenate([lower_keys, higher_keys], axis=0),
                jnp.concatenate([lower_values, higher_values], axis=0),
            )
    carry = initial
    for piece, first in pieces:
        sweep_carry = carry
        keys_all, values_all = piece
        sweep_count = keys_all.shape[0]
        size = 512
        whole = sweep_count // size * size
        if whole > 0:
            key_blocks = keys_all.reshape(whole // size, size, width)
            value_blocks = values_all.reshape(whole // size, size, width)
            firsts = first + jnp.arange(whole // size, dtype=jnp.int32) * size

            def step(state, items):
                return (attend(state, queries, q_ids, items[0], items[1], items[2], limit), None)

            sweep_carry, unused = lax.scan(step, sweep_carry, (key_blocks, value_blocks, firsts))
        if sweep_count > whole:
            sweep_carry = attend(
                sweep_carry, queries, q_ids, keys_all, values_all, first + whole, limit
            )
        carry = sweep_carry
    top_all, total_all, summed_all = carry
    result = (
        (summed_all / jnp.transpose(total_all)[:, :, None])
        .reshape(tok_rows, width)
        .astype(jnp.bfloat16)
    )
    return lax.all_to_all(result, "mp", split_axis=0, concat_axis=1, tiled=True)


def solution(mesh):
    in_specs = (P("seq", "mp"), P("seq", "mp"), P("seq", "mp"), P())
    out_specs = P(("seq", "mp"), None)
    return jax.shard_map(shards, mesh=mesh, in_specs=in_specs, out_specs=out_specs, check_vma=False)
```

profile of v0, /device:TPU:0, one launch (start us, length us, event | category | flops | bytes accessed | tf_op | source)
XLA Modules:
  0.0 105.4 jit_solution(15080296930586884671)
XLA Ops:
  0.0 1.4 %copy.86 = bf16[256,1536]{0,1:T(8,128)(2,1)S(1)} copy(bf16[256,1536]{1,0:T(8,128)(2,1)} %param.12) | data formatting | bytes 1572864 | tf_op args[2]
  2.0 1.4 %copy.85 = bf16[256,1536]{0,1:T(8,128)(2,1)S(1)} copy(bf16[256,1536]{1,0:T(8,128)(2,1)} %param.11) | data formatting | bytes 1572864 | tf_op args[1]
  3.9 1.8 %collective-permute-done = bf16[256,1536]{0,1:T(8,128)(2,1)S(1)} collective-permute-done((bf16[256,1536]{0,1:T(8,128)(2,1)S(1)}, bf16[256,1536]{0,1:T(8,128)(2,1)S(1)}, u32[]{:S(2)}, u32[]{:S(2)}) %collective-permute-start) | collective-permute-done | bytes 786464 | tf_op jit(solution)/shard_map/ppermute | solution.py:13
  6.6 1.3 %pad_maximum_fusion = bf16[512,1536]{0,1:T(8,128)(2,1)} fusion(bf16[256,1536]{0,1:T(8,128)(2,1)S(1)} %get-tuple-element.259, bf16[256,1536]{0,1:T(8,128)(2,1)S(1)} %get-tuple-element.260), kind=kLoop, calls=%fused_computation.54 | loop fusion | flops 3145728 | bytes 3145728 | tf_op jit(solution)/shard_map/concatenate | solution.py:94
  7.9 2.6 %collective-permute-start.2 = (bf16[512,1536]{0,1:T(8,128)(2,1)}, bf16[512,1536]{0,1:T(8,128)(2,1)}, u32[]{:S(2)}, u32[]{:S(2)}) collective-permute-start(bf16[512,1536]{0,1:T(8,128)(2,1)} %pad_maximum_fusion), channel_id=1, source_target_pairs={{0,4},{2,6},{4,0},{6,2},{8,12},{10,14},{12,8},{14,10},{16,20},{18,... | collective-permute-start | bytes 4718600 | tf_op jit(solution)/shard_map/ppermute | solution.py:13
  10.5 1.3 %pad_maximum_fusion.1 = bf16[512,1536]{0,1:T(8,128)(2,1)} fusion(bf16[256,1536]{0,1:T(8,128)(2,1)S(1)} %get-tuple-element.248, bf16[256,1536]{0,1:T(8,128)(2,1)S(1)} %get-tuple-element.247), kind=kLoop, calls=%fused_computation.55 | loop fusion | flops 3145728 | bytes 3145728 | tf_op jit(solution)/shard_map/concatenate | solution.py:95
  12.6 1.9 %and_reduce_fusion = pred[]{:T(512)} fusion(s32[]{:T(128)} %bitcast.11, s32[]{:T(128)} %bitcast.10, s32[256]{0:T(256)S(1)} %select_reduce_fusion.2, s32[]{:T(128)S(6)} %mul.101), kind=kLoop, calls=%fused_computation.81 | loop fusion | flops 5631 | bytes 1037 | tf_op jit(solution)/shard_map/reduce_or | solution.py:71
  15.1 1.9 %and_reduce_fusion.1 = (pred[]{:T(512)}, s32[256]{0:T(256)S(1)}) fusion(s32[]{:T(128)} %bitcast.11, s32[]{:T(128)} %bitcast.10, s32[256]{0:T(256)S(1)} %select_reduce_fusion.1, s32[]{:T(128)S(6)} %mul.105), kind=kLoop, calls=%fused_computation.82 | loop fusion | flops 5631 | bytes 2061 | tf_op jit(solution)/shard_map/reduce_or | solution.py:71
  17.8 1.9 %and_reduce_fusion.2 = (pred[]{:T(512)}, s32[512]{0:T(512)S(1)}) fusion(s32[]{:T(128)} %bitcast.11, s32[]{:T(128)} %bitcast.10, s32[512]{0:T(512)S(1)} %select_reduce_fusion, s32[]{:T(128)S(6)} %mul.97), kind=kLoop, calls=%fused_computation.84 | loop fusion | flops 11263 | bytes 4109 | tf_op jit(solution)/shard_map/while/body/eval_jaxpr/reduce_or | solution.py:71
  20.4 1.4 %copy.84 = bf16[256,1536]{0,1:T(8,128)(2,1)S(1)} copy(bf16[256,1536]{1,0:T(8,128)(2,1)} %param.10) | data formatting | bytes 1572864 | tf_op args[0]
  21.8 6.3 %conditional.3 = (f32[12,256]{1,0:T(8,128)}, f32[12,256]{1,0:T(8,128)S(1)}, f32[256,12,128]{2,0,1:T(8,128)S(1)}) conditional(s32[]{:T(128)} %convert_element_type.43, () %tuple.33, (s32[256]{0:T(256)S(1)}, bf16[256,12,128]{0,2,1:T(8,128)(2,1)S(1)}, bf16[256,12,128]{0,2,1:T(8,128)(2,1)S(1)}, bf16[256,12,128]{0,2,1:T(8,128)(2,1)S(1)}) %tuple.82), branch_computations={%region_10.11_spmd, %region_11.14_spmd} | conditional | flops 413347840 | bytes 16913460 | solution.py:72
  23.3 1.5 %fusion.2 = f32[12,256]{1,0:T(8,128)S(1)} fusion(f32[12,256,256]{1,2,0:T(8,128)S(1)} %get-tuple-element.246, f32[12,256]{1,0:T(8,128)} %get-tuple-element.264, pred[256,256]{0,1:T(8,128)(4,1)S(1)} %broadcast_compare_fusion), kind=kLoop, calls=%fused_computation.4 | loop fusion | flops 3929088 | bytes 3235840 | tf_op jit(solution)/shard_map/cond/branch_1_fun/reduce_sum | solution.py:60
  24.7 2.6 %bitcast_add_fusion = f32[256,12,128]{2,0,1:T(8,128)S(1)} fusion(bf16[256,12,128]{0,2,1:T(8,128)(2,1)} %copy-done.1, f32[12,256,256]{1,2,0:T(8,128)S(1)} %get-tuple-element.246, f32[12,256]{1,0:T(8,128)} %get-tuple-element.264, pred[256,256]{0,1:T(8,128)(4,1)S(1)} %broadcast_compare_fusion, f32[256,12]{0,1:T(8,128)S(1)} %get-tuple-element.231), kind=kOutput, calls=%fused_computation.6 | convolution fusion | flops 205651968 | bytes 5595136 | tf_op jit(solution)/shard_map/cond/branch_1_fun/hqk,khd->qhd/dot_general | solution.py:61
  28.1 6.2 %conditional.4 = ((f32[12,256]{1,0:T(8,128)}, f32[12,256]{1,0:T(8,128)S(1)}, f32[256,12,128]{2,0,1:T(8,128)S(1)})) conditional(s32[]{:T(128)} %convert_element_type.42, (f32[12,256]{1,0:T(8,128)}, f32[12,256]{1,0:T(8,128)S(1)}, f32[256,12,128]{2,0,1:T(8,128)S(1)}) %conditional.3, (s32[256]{0:T(256)S(1)}, s32[256]{0:T(256)S(1)}, ...), branch_computations={%region_14.15_spmd, %region_15.18_spmd} | conditional | flops 413737984 | bytes 15403040 | solution.py:72
  28.2 1.8 %fusion.17 = (f32[12,256]{1,0:T(8,128)S(1)}, f32[12,256,256]{1,2,0:T(8,128)S(1)}) fusion(pred[256,256]{0,1:T(8,128)(4,1)S(1)} %broadcast_compare_fusion.1, bf16[256,12,128]{0,2,1:T(8,128)(2,1)S(1)} %get-tuple-element.216, bf16[256,12,128]{0,2,1:T(8,128)(2,1)} %bitcast.40), kind=kOutput, calls=%fused_computation.22 | convolution fusion | flops 203682816 | bytes 4796416 | tf_op jit(solution)/shard_map/cond/branch_1_fun/qhd,khd->hqk/dot_general | solution.py:53
  30.8 1.4 %bitcast_add_fusion.1 = f32[256,12,128]{2,0,1:T(8,128)S(1)} fusion(f32[256,12,128]{2,0,1:T(8,128)S(1)} %get-tuple-element.123, bf16[256,12,128]{0,2,1:T(8,128)(2,1)S(1)} %bitcast.43, f32[12,256,256]{1,2,0:T(8,128)S(1)} %get-tuple-element.242, f32[12,256]{1,0:T(8,128)S(1)} %get-tuple-element.270, pred[256,256]{0,1:T(8,128)(4,1)S(1)} %broadcast_compare_fusion.1, ...), kind=kOutput, calls=%fused_computation.26 | convolution fusion | flops 206045184 | bytes 7168000 | tf_op jit(solution)/shard_map/cond/branch_1_fun/hqk,khd->qhd/dot_general | solution.py:61
  34.3 11.8 %collective-permute-done.2 = bf16[512,1536]{0,1:T(8,128)(2,1)} collective-permute-done((bf16[512,1536]{0,1:T(8,128)(2,1)}, bf16[512,1536]{0,1:T(8,128)(2,1)}, u32[]{:S(2)}, u32[]{:S(2)}) %collective-permute-start.2) | collective-permute-done | bytes 1572896 | tf_op jit(solution)/shard_map/ppermute | solution.py:13
  46.1 33.4 %collective-permute-done.3 = bf16[512,1536]{0,1:T(8,128)(2,1)} collective-permute-done((bf16[512,1536]{0,1:T(8,128)(2,1)}, bf16[512,1536]{0,1:T(8,128)(2,1)}, u32[]{:S(2)}, u32[]{:S(2)}) %collective-permute-start.3) | collective-permute-done | bytes 1572896 | tf_op jit(solution)/shard_map/ppermute | solution.py:13
  79.5 10.2 %conditional.5 = ((f32[12,256]{1,0:T(8,128)S(1)}, f32[256,12,128]{2,0,1:T(8,128)S(1)})) conditional(s32[]{:T(128)} %convert_element_type.40, (f32[12,256]{1,0:T(8,128)S(1)}, f32[256,12,128]{2,0,1:T(8,128)S(1)}) %tuple.36, (s32[256]{0:T(256)S(1)}, s32[512]{0:T(512)S(1)}, bf16[512,1536]{0,1:T(8,128)(2,1)}, bf16[256,12,128]{0,2,1:T(8,128)(2,1)S(1)}, ...), branch_computations={%region_18.19_spmd, %region_19.22_spmd} | conditional | flops 826680320 | bytes 26651672 | solution.py:72
  79.6 2.8 %fusion.33 = (f32[12,256]{1,0:T(8,128)S(1)}, f32[12,256,512]{2,1,0:T(8,128)S(1)}) fusion(pred[256,512]{1,0:T(8,128)(4,1)S(1)} %broadcast_compare_fusion.2, bf16[256,12,128]{0,2,1:T(8,128)(2,1)S(1)} %get-tuple-element.224, bf16[512,12,128]{0,2,1:T(8,128)(2,1)} %bitcast.6), kind=kOutput, calls=%fused_computation.41 | convolution fusion | flops 407368704 | bytes 8794112 | tf_op jit(solution)/shard_map/while/body/eval_jaxpr/cond/branch_1_fun/qhd,khd->hqk/dot_general | solution.py:53
  83.1 3.8 %bitcast_add_fusion.2 = f32[256,12,128]{2,0,1:T(8,128)S(1)} fusion(f32[256,12,128]{2,0,1:T(8,128)S(1)} %get-tuple-element.131, bf16[512,12,128]{0,2,1:T(8,128)(2,1)} %bitcast.8, f32[12,256,512]{2,1,0:T(8,128)S(1)} %get-tuple-element.244, f32[12,256]{1,0:T(8,128)S(1)} %get-tuple-element.236, pred[256,512]{1,0:T(8,128)(4,1)S(1)} %broadcast_compare_fusion.2, ...), kind=kOutput, calls=%fused_computation.46 | convolution fusion | flops 411303936 | bytes 11165696 | tf_op jit(solution)/shard_map/while/body/eval_jaxpr/cond/branch_1_fun/hqk,khd->qhd/dot_general | solution.py:61
  87.0 2.0 %fusion.35 = f32[12,256]{1,0:T(8,128)S(1)} fusion(f32[12,256,512]{2,1,0:T(8,128)S(1)} %get-tuple-element.244, f32[12,256]{1,0:T(8,128)S(1)} %get-tuple-element.236, pred[256,512]{1,0:T(8,128)(4,1)S(1)} %broadcast_compare_fusion.2), kind=kLoop, calls=%fused_computation.43 | loop fusion | flops 7861248 | bytes 6447104 | tf_op jit(solution)/shard_map/while/body/eval_jaxpr/cond/branch_1_fun/reduce_sum | solution.py:60
  90.8 13.5 %all_to_all.16 = bf16[2,128,1536]{1,2,0:T(8,128)(2,1)S(1)} all-to-all(bf16[2,128,1536]{1,2,0:T(8,128)(2,1)S(1)} %copy.99), channel_id=1, replica_groups=mesh['seq'=16,'mp'=2] {'mp'}, dimensions={0} | all-to-all | bytes 1572864 | tf_op jit(solution)/shard_map/all_to_all | solution.py:124
  104.2 1.2 %copy.100 = bf16[128,3072]{1,0:T(8,128)(2,1)} copy(bf16[128,3072]{0,1:T(8,128)(2,1)S(1)} %bitcast.42) | data formatting | bytes 1572864 | tf_op jit(solution)/shard_map/all_to_all | solution.py:124
  (38 shorter events, 10.5 us)
Async XLA Ops:
  0.0 3.5 %copy-start.2 = (s32[4,4]{1,0:T(4,128)S(1)}, s32[4,4]{1,0:T(4,128)}, u32[]{:S(2)}) copy-start(s32[4,4]{1,0:T(4,128)} %param.13) | copy-start | bytes 196
  1.4 2.5 %collective-permute-start.1 = (bf16[256,1536]{0,1:T(8,128)(2,1)S(1)}, bf16[256,1536]{0,1:T(8,128)(2,1)S(1)}, u32[]{:S(2)}, u32[]{:S(2)}) collective-permute-start(bf16[256,1536]{0,1:T(8,128)(2,1)S(1)} %copy.86), channel_id=1, source_target_pairs={{0,2},{2,0},{4,6},{6,4},{8,10},{10,8},{12,14},{14,12},{16,18},{18,... | collective-permute-start | bytes 2359304 | tf_op jit(solution)/shard_map/ppermute | solution.py:13
  3.4 2.4 %collective-permute-start = (bf16[256,1536]{0,1:T(8,128)(2,1)S(1)}, bf16[256,1536]{0,1:T(8,128)(2,1)S(1)}, u32[]{:S(2)}, u32[]{:S(2)}) collective-permute-start(bf16[256,1536]{0,1:T(8,128)(2,1)S(1)} %copy.85), channel_id=1, source_target_pairs={{0,2},{2,0},{4,6},{6,4},{8,10},{10,8},{12,14},{14,12},{16,18},{18,... | collective-permute-start | bytes 2359304 | tf_op jit(solution)/shard_map/ppermute | solution.py:13
  5.7 0.9 copy-start
  7.9 38.2 %collective-permute-start.2 = (bf16[512,1536]{0,1:T(8,128)(2,1)}, bf16[512,1536]{0,1:T(8,128)(2,1)}, u32[]{:S(2)}, u32[]{:S(2)}) collective-permute-start(bf16[512,1536]{0,1:T(8,128)(2,1)} %pad_maximum_fusion), channel_id=1, source_target_pairs={{0,4},{2,6},{4,0},{6,2},{8,12},{10,14},{12,8},{14,10},{16,20},{18,... | collective-permute-start | bytes 4718600 | tf_op jit(solution)/shard_map/ppermute | solution.py:13
  11.8 67.7 %collective-permute-start.3 = (bf16[512,1536]{0,1:T(8,128)(2,1)}, bf16[512,1536]{0,1:T(8,128)(2,1)}, u32[]{:S(2)}, u32[]{:S(2)}) collective-permute-start(bf16[512,1536]{0,1:T(8,128)(2,1)} %pad_maximum_fusion.1), channel_id=1, source_target_pairs={{0,4},{2,6},{4,0},{6,2},{8,12},{10,14},{12,8},{14,10},{16,20},{18,... | collective-permute-start | bytes 4718600 | tf_op jit(solution)/shard_map/ppermute | solution.py:13
  21.8 1.4 %copy-start.1 = (bf16[256,12,128]{0,2,1:T(8,128)(2,1)}, bf16[256,12,128]{0,2,1:T(8,128)(2,1)S(1)}, u32[]{:S(2)}) copy-start(bf16[256,12,128]{0,2,1:T(8,128)(2,1)S(1)} %get-tuple-element.212) | copy-start | bytes 2359300 | tf_op jit(solution)/shard_map/cond
where the time goes:
time: 106 us; the launch traced here: 105 us
  waiting for transfers between devices  47.1 us (44%)
  other arithmetic  18.3 us (17%)
  blocking collectives  13.5 us (13%)
  matrix products  13.2 us (12%)
  local copies, waits for them, and re-layouts  7.83 us (7%)
  starting transfers between devices  3.28 us (3%)
  between operations  2.06 us (2%)
    ppermute x4, waiting for transfers between devices, from_partner(): lax.ppermute(array, axis, [(i, i ^ 1 << apart) for i in range(lax.axis_si...  47.1 us
    all_to_all x1, blocking collectives, shards(): return lax.all_to_all(result, 'mp', split_axis=0, concat_axis=1, tiled=True)  13.5 us
    dot_general x3, matrix products, update(): jnp.einsum('hqk,khd->qhd', weight.astype(jnp.bfloat16), values, preferred...  7.81 us
    reduce_or x3, other arithmetic, attend(): needed = needed & jnp.any((k_ids >= q_clip[0]) & (k_ids <= q_clip[-1]))  5.74 us
    dot_general x3, matrix products, update(): jnp.einsum('qhd,khd->hqk', q_rows, keys, preferred_element_type=jnp.float32)  5.35 us
    unnamed x7, local copies, waits for them, and re-layouts  4.89 us
    reduce_sum x3, other arithmetic, update(): total_new = total_old * factor + jnp.sum(weight, axis=-1)  4.23 us
    ppermute x4, starting transfers between devices, from_partner(): lax.ppermute(array, axis, [(i, i ^ 1 << apart) for i in range(lax.axis_si...  3.28 us
  transfers between devices with their start and end apart: 4, of which 4 were waited for; matrix products, arithmetic and copies ran while one was open for 22% of the time, Pallas kernels for 0%

commit v1 on v0

v1 whole, which is shorter than its diff:
```python
import functools

import jax
import jax.numpy as jnp
from jax import lax
from jax.experimental import pallas as pl
from jax.experimental.pallas import tpu as pltpu
from jax.sharding import PartitionSpec as P

HD = 128
NEG = -1e30
LOG2E = 1.4426950408889634
MESH = pl.DeviceIdType.MESH


def kernel(
    group, pair, mp, heads,
    lengths, query, key, value, out,
    q_buf, k_buf, v_buf, o_buf,
    q_in, k_in, v_in, o_in, q_out, k_out, v_out, o_out,
):
    rows = query.shape[0]
    part = rows // mp
    per_core = heads // pair
    others = group // pair
    slots = lengths.shape[1]
    seq_index = lax.axis_index("seq")
    mp_index = lax.axis_index("mp")
    bucket = seq_index // group
    place = lax.rem(seq_index, group)
    core = lax.rem(place, pair)
    chip = place // pair

    def peer(chip_step, core_step):
        there_chip = lax.rem(chip + chip_step, others)
        there_core = lax.rem(core + core_step, pair)
        return there_chip, there_core, bucket * group + there_chip * pair + there_core

    def columns(owner, head):
        return pl.ds(pl.multiple_of((owner * per_core + head) * HD, HD), HD)

    def slot(index):
        return pl.ds(pl.multiple_of(index * rows, rows), rows)

    def local_copies(head):
        mine = columns(core, head)
        return (
            pltpu.make_async_copy(query.at[:, mine], q_buf.at[head, slot(core), :], q_in.at[head, core]),
            pltpu.make_async_copy(key.at[:, mine], k_buf.at[head, slot(place), :], k_in.at[head, place]),
            pltpu.make_async_copy(value.at[:, mine], v_buf.at[head, slot(place), :], v_in.at[head, place]),
        )

    def sends(head, chip_step, core_step):
        there_chip, there_core, there_seq = peer(chip_step, core_step)
        theirs = columns(there_core, head)
        target = {"seq": there_seq, "mp": mp_index}
        index = chip_step * pair + core_step
        copies = [
            pltpu.make_async_remote_copy(
                src_ref=source.at[:, theirs], dst_ref=buf.at[head, slot(place), :],
                send_sem=left.at[head, index], recv_sem=landed.at[head, place],
                device_id=target, device_id_type=MESH,
            )
            for source, buf, left, landed in (
                (key, k_buf, k_out, k_in), (value, v_buf, v_out, v_in),
            )
        ]
        if chip_step == 0:
            copies.insert(0, pltpu.make_async_remote_copy(
                src_ref=query.at[:, theirs], dst_ref=q_buf.at[head, slot(core), :],
                send_sem=q_out.at[head, index], recv_sem=q_in.at[head, core],
                device_id=target, device_id_type=MESH,
            ))
        return copies

    def results(head, core_step, mp_step):
        there_core = lax.rem(core + core_step, pair)
        there_mp = lax.rem(mp_index + mp_step, mp)
        source = o_buf.at[head, pl.ds(pl.multiple_of(there_core * rows + there_mp * part, part), part), :]
        place_out = out.at[:, pl.ds(pl.multiple_of((mp_index * heads + core * per_core + head) * HD, HD), HD)]
        index = core_step * mp + mp_step
        if index == 0:
            return pltpu.make_async_copy(source, place_out, o_in.at[head, 0])
        return pltpu.make_async_remote_copy(
            src_ref=source, dst_ref=place_out,
            send_sem=o_out.at[head, index], recv_sem=o_in.at[head, index],
            device_id={"seq": bucket * group + chip * pair + there_core, "mp": there_mp},
            device_id_type=MESH,
        )

    far = [(a, b) for b in range(pair) for a in range(1, others)]
    near = [(0, b) for b in range(1, pair)]
    to_owner = [(b, m) for m in range(mp) for b in range(pair)]

    barrier = pltpu.get_barrier_semaphore()
    for chip_step, core_step in far + near:
        there_seq = peer(chip_step, core_step)[2]
        pl.semaphore_signal(barrier, inc=1, device_id={"seq": there_seq, "mp": mp_index}, device_id_type=MESH)
    for core_step, mp_step in to_owner:
        if mp_step > 0:
            pl.semaphore_signal(
                barrier, inc=1,
                device_id={"seq": peer(0, core_step)[2], "mp": lax.rem(mp_index + mp_step, mp)},
                device_id_type=MESH,
            )

    @pl.loop(0, per_core)
    def _(head):
        for copy in local_copies(head):
            copy.start()

    ends = []
    running = jnp.int32(0)
    for i in range(slots):
        running = running + lengths[bucket, i]
        ends.append(running)

    def ids(offset):
        found = jnp.zeros_like(offset)
        for end in ends:
            found = found + (offset >= end).astype(jnp.int32)
        return found

    k_ids = ids(lax.broadcasted_iota(jnp.int32, (1, group * rows), 1))

    pl.semaphore_wait(barrier, len(far) + len(near) + (mp - 1) * pair)

    @pl.loop(0, per_core)
    def _(head):
        together = [sends(head, *step) for step in far]
        for kind in range(2):
            for copies in together:
                copies[kind].start()
        for step in near:
            for copy in sends(head, *step):
                copy.start()

    def arrived(buf, sem, head, count):
        for i in range(count):
            ref = buf.at[head, pl.ds(i * rows, rows), :]
            pltpu.make_async_copy(ref, ref, sem.at[head, i]).wait()

    factor = LOG2E / HD**0.5

    @pl.loop(0, per_core)
    def _(head):
        arrived(q_buf, q_in, head, pair)
        arrived(k_buf, k_in, head, group)
        arrived(v_buf, v_in, head, group)
        keys = k_buf[head]
        values = v_buf[head]
        for b in range(pair):
            q_rows = q_buf[head, pl.ds(b * rows, rows), :]
            q_ids = ids(lax.broadcasted_iota(jnp.int32, (rows, 1), 0) + (chip * pair + b) * rows)
            score = lax.dot_general(
                q_rows, keys, (((1,), (1,)), ((), ())), preferred_element_type=jnp.float32
            )
            score = jnp.where(q_ids == k_ids, score, NEG)
            top = jnp.max(score, axis=1, keepdims=True)
            weight = jnp.exp2((score - top) * factor)
            total = jnp.sum(weight, axis=1, keepdims=True)
            summed = jnp.dot(weight.astype(jnp.bfloat16), values, preferred_element_type=jnp.float32)
            o_buf[head, pl.ds(b * rows, rows), :] = (summed / total).astype(jnp.bfloat16)
        for step in reversed(to_owner):
            results(head, *step).start()

    @pl.loop(0, per_core)
    def _(head):
        for step in far + near:
            for copy in sends(head, *step):
                copy.wait_send()
        for step in to_owner:
            if step == (0, 0):
                results(head, *step).wait()
            else:
                results(head, *step).wait_send()
                results(head, *step).wait_recv()


def shards(query, key, value, clip_lengths):
    rows, width = query.shape
    heads = width // HD
    group = lax.axis_size("seq") // clip_lengths.shape[0]
    mp = lax.axis_size("mp")
    pair = 2 if group % 2 == 0 and heads % 2 == 0 else 1
    per_core = heads // pair
    dma = pltpu.SemaphoreType.DMA
    whole = pl.BlockSpec(memory_space=pl.ANY)
    return pl.pallas_call(
        functools.partial(kernel, group, pair, mp, heads),
        out_shape=jax.ShapeDtypeStruct((rows // mp, width * mp), jnp.bfloat16),
        in_specs=[pl.BlockSpec(memory_space=pltpu.SMEM), whole, whole, whole],
        out_specs=pl.BlockSpec(memory_space=pltpu.VMEM),
        scratch_shapes=[
            pltpu.VMEM((per_core, pair * rows, HD), jnp.bfloat16),
            pltpu.VMEM((per_core, group * rows, HD), jnp.bfloat16),
            pltpu.VMEM((per_core, group * rows, HD), jnp.bfloat16),
            pltpu.VMEM((per_core, pair * rows, HD), jnp.bfloat16),
            dma((per_core, pair)), dma((per_core, group)), dma((per_core, group)), dma((per_core, pair * mp)),
            dma((per_core, pair)), dma((per_core, group)), dma((per_core, group)), dma((per_core, pair * mp)),
        ],
        compiler_params=pltpu.CompilerParams(collective_id=0, has_side_effects=True),
        name="packed_attention",
    )(clip_lengths, query, key, value)


def solution(mesh):
    in_specs = (P("seq", "mp"), P("seq", "mp"), P("seq", "mp"), P())
    out_specs = P(("seq", "mp"), None)
    return jax.shard_map(shards, mesh=mesh, in_specs=in_specs, out_specs=out_specs, check_vma=False)
```

time: 106 us -> 48.5 us (0.46)
  waiting for transfers between devices: 47.1 us -> 0 us
  Pallas kernels: 0 us -> 46.3 us
  other arithmetic: 18.3 us -> 0 us
  blocking collectives: 13.5 us -> 0 us
  matrix products: 13.2 us -> 0 us
  local copies, waits for them, and re-layouts: 7.83 us -> 2.06 us
  starting transfers between devices: 3.28 us -> 0 us
  between operations: 2.06 us -> 0.01 us
    ppermute x4 -> x0, waiting for transfers between devices: 47.1 us -> none  [from_partner(): lax.ppermute(array, axis, [(i, i ^ 1 << apart) for i in range(lax.axis_si...]
    pallas_call x0 -> x1, Pallas kernels: none -> 46.3 us  [shards(): pl.pallas_call(functools.partial(kernel, group, pair, mp, heads), out_sha...]
    all_to_all x1 -> x0, blocking collectives: 13.5 us -> none  [shards(): return lax.all_to_all(result, 'mp', split_axis=0, concat_axis=1, tiled=True)]
    dot_general x6 -> x0, matrix products: 13.2 us -> none  [the longest x3 7.81 us: update(): jnp.einsum('hqk,khd->qhd', weight.astype(jnp.bfloat16), values, preferred...]
    reduce_or x3 -> x0, other arithmetic: 5.74 us -> none  [attend(): needed = needed & jnp.any((k_ids >= q_clip[0]) & (k_ids <= q_clip[-1]))]
    reduce_sum x8 -> x0, other arithmetic: 4.49 us -> none  [the longest x3 4.23 us: update(): total_new = total_old * factor + jnp.sum(weight, axis=-1)]
    ppermute x4 -> x0, starting transfers between devices: 3.28 us -> none  [from_partner(): lax.ppermute(array, axis, [(i, i ^ 1 << apart) for i in range(lax.axis_si...]
    unnamed x7 -> x1, local copies, waits for them, and re-layouts: 4.89 us -> 2.06 us
  transfers between devices with their start and end apart: 4 -> 0, of which waited for: 4 -> 0; matrix products, arithmetic and copies ran while one was open for 22% -> 0% of each run, Pallas kernels for 0% -> 0%
where the time goes in v1:
time: 48.5 us; the launch traced here: 48.3 us
  Pallas kernels  46.3 us (95%)
  local copies, waits for them, and re-layouts  2.06 us (4%)
    pallas_call x1, Pallas kernels, shards(): pl.pallas_call(functools.partial(kernel, group, pair, mp, heads), out_sha...  46.3 us
    unnamed x1, local copies, waits for them, and re-layouts  2.06 us

profile of v1, /device:TPU:0, one launch (start us, length us, event | category | flops | bytes accessed | tf_op | source)
XLA Modules:
  0.0 48.3 jit_solution(4938057299761803408)
XLA Ops:
  0.0 46.3 %packed_attention.1 = bf16[128,3072]{1,0:T(8,128)(2,1)} custom-call(s32[4,4]{1,0:T(4,128)} %lengths.1, bf16[256,1536]{1,0:T(8,128)(2,1)} %query.1, bf16[256,1536]{1,0:T(8,128)(2,1)} %key.1, bf16[256,1536]{1,0:T(8,128)(2,1)} %value.1), custom_call_target="tpu_custom_call" | custom-call | tf_op jit(solution)/shard_map/packed_attention/pallas_call | solution.py:189
  46.3 2.1 %copy.6 = bf16[128,3072]{1,0:T(8,128)(2,1)} copy(bf16[128,3072]{1,0:T(8,128)(2,1)} %packed_attention.1) | data formatting | bytes 1572864

commit v2 on v1

v2 whole, which is shorter than its diff:
```python
import functools

import jax
import jax.numpy as jnp
from jax import lax
from jax.experimental import pallas as pl
from jax.experimental.pallas import tpu as pltpu
from jax.sharding import PartitionSpec as P

HD = 128
NEG = -1e30
LOG2E = 1.4426950408889634
MESH = pl.DeviceIdType.MESH


def kernel(
    group, pair, mp, heads,
    lengths, query, key, value, out,
    q_buf, k_buf, v_buf, o_buf, k_first, v_first, p_buf, t_buf,
    q_in, k_in, v_in, o_in, q_out, k_out, v_out, o_out, first_in,
):
    rows = query.shape[0]
    part = rows // mp
    per_core = heads // pair
    others = group // pair
    slots = lengths.shape[1]
    seq_index = lax.axis_index("seq")
    mp_index = lax.axis_index("mp")
    bucket = seq_index // group
    place = lax.rem(seq_index, group)
    core = lax.rem(place, pair)
    chip = place // pair

    def seq_of(chip_step, there_core):
        return bucket * group + lax.rem(chip + chip_step, others) * pair + there_core

    def columns(owner, head):
        return pl.ds(pl.multiple_of((owner * per_core + head) * HD, HD), HD)

    def slot(index):
        return pl.ds(pl.multiple_of(index * rows, rows), rows)

    def local_copies(head):
        mine = columns(core, head)
        return (
            pltpu.make_async_copy(query.at[:, mine], q_buf.at[head, slot(core), :], q_in.at[head, core]),
            pltpu.make_async_copy(key.at[:, mine], k_buf.at[head, slot(place), :], k_in.at[head, place]),
            pltpu.make_async_copy(value.at[:, mine], v_buf.at[head, slot(place), :], v_in.at[head, place]),
        )

    def first_copies(there_core):
        theirs = columns(there_core, 0)
        return (
            pltpu.make_async_copy(key.at[:, theirs], k_first.at[there_core], first_in.at[0, there_core]),
            pltpu.make_async_copy(value.at[:, theirs], v_first.at[there_core], first_in.at[1, there_core]),
        )

    def send(head, chip_step, there_core, kind, staged=None):
        source, buf, left, landed = (
            (query, q_buf, q_out, q_in), (key, k_buf, k_out, k_in), (value, v_buf, v_out, v_in)
        )[kind]
        at = core if kind == 0 else place
        index = there_core if kind == 0 else chip_step * pair + there_core
        return pltpu.make_async_remote_copy(
            src_ref=source.at[:, columns(there_core, head)] if staged is None else staged.at[there_core],
            dst_ref=buf.at[head, slot(at), :],
            send_sem=left.at[head, index], recv_sem=landed.at[head, at],
            device_id={"seq": seq_of(chip_step, there_core), "mp": mp_index}, device_id_type=MESH,
        )

    def far_sends(head, staged=(None, None, None)):
        return [
            send(head, chip_step, there_core, kind, staged[kind])
            for kind in (1, 2) for there_core in range(pair) for chip_step in range(1, others)
        ]

    def near_sends(head):
        return [
            send(head, 0, lax.rem(core + step, pair), kind)
            for kind in range(3) for step in range(1, pair)
        ]

    def results(head, core_step, mp_step):
        there_core = lax.rem(core + core_step, pair)
        there_mp = lax.rem(mp_index + mp_step, mp)
        source = o_buf.at[head, pl.ds(pl.multiple_of(there_core * rows + there_mp * part, part), part), :]
        place_out = out.at[:, pl.ds(pl.multiple_of((mp_index * heads + core * per_core + head) * HD, HD), HD)]
        index = core_step * mp + mp_step
        if index == 0:
            return pltpu.make_async_copy(source, place_out, o_in.at[head, 0])
        return pltpu.make_async_remote_copy(
            src_ref=source, dst_ref=place_out,
            send_sem=o_out.at[head, index], recv_sem=o_in.at[head, index],
            device_id={"seq": seq_of(0, there_core), "mp": there_mp}, device_id_type=MESH,
        )

    for there_core in range(pair):
        for copy in first_copies(there_core):
            copy.start()

    barrier = pltpu.get_barrier_semaphore()
    greeted = [(seq_of(a, b), mp_index) for a in range(1, others) for b in range(pair)]
    greeted += [(seq_of(0, lax.rem(core + b, pair)), mp_index) for b in range(1, pair)]
    greeted += [(seq_of(0, b), lax.rem(mp_index + m, mp)) for b in range(pair) for m in range(1, mp)]
    for there_seq, there_mp in greeted:
        pl.semaphore_signal(
            barrier, inc=1, device_id={"seq": there_seq, "mp": there_mp}, device_id_type=MESH
        )

    @pl.loop(0, per_core)
    def _(head):
        for copy in local_copies(head):
            copy.start()

    ends = []
    running = jnp.int32(0)
    for i in range(slots):
        running = running + lengths[bucket, i]
        ends.append(running)

    def ids(offset):
        found = jnp.zeros_like(offset)
        for end in ends:
            found = found + (offset >= end).astype(jnp.int32)
        return found

    k_ids = ids(lax.broadcasted_iota(jnp.int32, (1, group * rows), 1))

    for there_core in range(pair):
        for copy in first_copies(there_core):
            copy.wait()
    pl.semaphore_wait(barrier, len(greeted))

    for copy in far_sends(0, (None, k_first, v_first)) + near_sends(0):
        copy.start()

    @pl.loop(1, per_core)
    def _(head):
        for copy in far_sends(head) + near_sends(head):
            copy.start()

    def arrived(buf, sem, head, count):
        for i in range(count):
            ref = buf.at[head, pl.ds(i * rows, rows), :]
            pltpu.make_async_copy(ref, ref, sem.at[head, i]).wait()

    factor = LOG2E / HD**0.5

    def settle(head):
        for step in range(pair * mp):
            copy = results(head, step // mp, step % mp)
            if step == 0:
                copy.wait()
            else:
                copy.wait_send()
                copy.wait_recv()

    @pl.loop(0, per_core)
    def _(head):
        arrived(q_buf, q_in, head, pair)
        arrived(k_buf, k_in, head, group)
        keys = k_buf[head]
        for b in range(pair):
            block = pl.ds(b * rows, rows)
            q_ids = ids(lax.broadcasted_iota(jnp.int32, (rows, 1), 0) + (chip * pair + b) * rows)
            score = lax.dot_general(
                q_buf[head, block, :], keys, (((1,), (1,)), ((), ())), preferred_element_type=jnp.float32
            )
            score = jnp.where(q_ids == k_ids, score, NEG)
            top = jnp.max(score, axis=1, keepdims=True)
            weight = jnp.exp2((score - top) * factor)
            t_buf[block, :] = jnp.broadcast_to(jnp.sum(weight, axis=1, keepdims=True), (rows, HD))
            p_buf[block, :] = weight.astype(jnp.bfloat16)
        arrived(v_buf, v_in, head, group)
        for core_step in reversed(range(pair)):
            block = slot(lax.rem(core + core_step, pair))
            summed = jnp.dot(p_buf[block, :], v_buf[head], preferred_element_type=jnp.float32)
            o_buf[head, block, :] = (summed / t_buf[block, :]).astype(jnp.bfloat16)
            for mp_step in reversed(range(mp)):
                results(head, core_step, mp_step).start()
        for copy in far_sends(head) + near_sends(head):
            copy.wait_send()

        @pl.when(head > 0)
        def _():
            settle(head - 1)

    settle(per_core - 1)


def shards(query, key, value, clip_lengths):
    rows, width = query.shape
    heads = width // HD
    group = lax.axis_size("seq") // clip_lengths.shape[0]
    mp = lax.axis_size("mp")
    pair = 2 if group % 2 == 0 and heads % 2 == 0 else 1
    per_core = heads // pair
    dma = pltpu.SemaphoreType.DMA
    whole = pl.BlockSpec(memory_space=pl.ANY)
    return pl.pallas_call(
        functools.partial(kernel, group, pair, mp, heads),
        out_shape=pltpu.VMEM((rows // mp, width * mp), jnp.bfloat16),
        in_specs=[pl.BlockSpec(memory_space=pltpu.SMEM), whole, whole, whole],
        out_specs=pl.BlockSpec(memory_space=pltpu.VMEM),
        scratch_shapes=[
            pltpu.VMEM((per_core, pair * rows, HD), jnp.bfloat16),
            pltpu.VMEM((per_core, group * rows, HD), jnp.bfloat16),
            pltpu.VMEM((per_core, group * rows, HD), jnp.bfloat16),
            pltpu.VMEM((per_core, pair * rows, HD), jnp.bfloat16),
            pltpu.VMEM((pair, rows, HD), jnp.bfloat16),
            pltpu.VMEM((pair, rows, HD), jnp.bfloat16),
            pltpu.VMEM((pair * rows, group * rows), jnp.bfloat16),
            pltpu.VMEM((pair * rows, HD), jnp.float32),
            dma((per_core, pair)), dma((per_core, group)), dma((per_core, group)), dma((per_core, pair * mp)),
            dma((per_core, pair)), dma((per_core, group)), dma((per_core, group)), dma((per_core, pair * mp)),
            dma((2, pair)),
        ],
        compiler_params=pltpu.CompilerParams(collective_id=0, has_side_effects=True),
        name="packed_attention",
    )(clip_lengths, query, key, value)


def solution(mesh):
    in_specs = (P("seq", "mp"), P("seq", "mp"), P("seq", "mp"), P())
    out_specs = P(("seq", "mp"), None)
    return jax.shard_map(shards, mesh=mesh, in_specs=in_specs, out_specs=out_specs, check_vma=False)
```

time: 48.5 us -> 45.5 us (0.938)
  Pallas kernels: 46.3 us -> 44.4 us
  local copies, waits for them, and re-layouts: 2.06 us -> 0.88 us
    pallas_call x1, Pallas kernels: 46.3 us -> 44.4 us  [shards(): pl.pallas_call(functools.partial(kernel, group, pair, mp, heads), out_sha...]
    unnamed x1, local copies, waits for them, and re-layouts: 2.06 us -> 0.88 us
where the time goes in v2:
time: 45.5 us; the launch traced here: 45.3 us
  Pallas kernels  44.4 us (98%)
  local copies, waits for them, and re-layouts  0.88 us (2%)
    pallas_call x1, Pallas kernels, shards(): pl.pallas_call(functools.partial(kernel, group, pair, mp, heads), out_sha...  44.4 us

profile of v2, /device:TPU:0, one launch (start us, length us, event | category | flops | bytes accessed | tf_op | source)
XLA Modules:
  0.0 45.3 jit_solution(6218428836728175841)
XLA Ops:
  0.0 44.4 %packed_attention.1 = bf16[128,3072]{1,0:T(8,128)(2,1)S(1)} custom-call(s32[4,4]{1,0:T(4,128)} %lengths.1, bf16[256,1536]{1,0:T(8,128)(2,1)} %query.1, bf16[256,1536]{1,0:T(8,128)(2,1)} %key.1, bf16[256,1536]{1,0:T(8,128)(2,1)} %value.1), custom_call_target="tpu_custom_call" | custom-call | tf_op jit(solution)/shard_map/packed_attention/pallas_call | solution.py:200
  44.4 0.9 %copy.6 = bf16[128,3072]{1,0:T(8,128)(2,1)} copy(bf16[128,3072]{1,0:T(8,128)(2,1)S(1)} %packed_attention.1) | data formatting | bytes 1572864

commit v3 on v2

v3 whole, which is shorter than its diff:
```python
import functools

import jax
import jax.numpy as jnp
from jax import lax
from jax.experimental import pallas as pl
from jax.experimental.pallas import tpu as pltpu
from jax.sharding import PartitionSpec as P

HD = 128
NEG = -1e30
LOG2E = 1.4426950408889634
MESH = pl.DeviceIdType.MESH


def kernel(
    group, pair, mp, heads, extra,
    lengths, query, key, value, out,
    q_buf, k_buf, v_buf, o_buf, first, p_buf, t_buf,
    q_in, k_in, v_in, o_in, q_out, k_out, v_out, o_out, first_in, ready,
):
    rows = query.shape[0]
    part = rows // mp
    per_core = heads // pair
    others = group // pair
    held = per_core - extra
    slots = lengths.shape[1]
    seq_index = lax.axis_index("seq")
    mp_index = lax.axis_index("mp")
    bucket = seq_index // group
    place = lax.rem(seq_index, group)
    core = lax.rem(place, pair)
    chip = place // pair

    def chip_at(chip_step):
        return lax.rem(chip + chip_step, others)

    def seq_of(chip_step, there_core):
        return bucket * group + chip_at(chip_step) * pair + there_core

    def head_of(slot, there_chip):
        if extra and isinstance(slot, int) and slot == 0:
            return there_chip
        return slot + extra

    def columns(owner, head):
        return pl.ds(pl.multiple_of((owner * per_core + head) * HD, HD), HD)

    def block_at(index):
        return pl.ds(pl.multiple_of(index * rows, rows), rows)

    kinds = ((query, q_buf, q_out, q_in), (key, k_buf, k_out, k_in), (value, v_buf, v_out, v_in))

    def local_copies(slot):
        mine = columns(core, head_of(slot, chip))
        return [
            pltpu.make_async_copy(source.at[:, mine], buf.at[slot, block_at(place), :], landed.at[slot, place])
            for source, buf, left, landed in kinds
        ]

    def far_kinds(slot):
        whole = extra and isinstance(slot, int) and slot == 0
        return (0, 1, 2) if whole else (1, 2)

    far = [(chip_step, there_core) for there_core in range(pair) for chip_step in range(1, others)]

    def first_copies():
        return [
            pltpu.make_async_copy(
                kinds[kind][0].at[:, columns(there_core, head_of(0, chip_at(chip_step)))],
                first.at[kind, chip_step * pair + there_core],
                first_in.at[kind, chip_step * pair + there_core],
            )
            for kind in far_kinds(0) for chip_step, there_core in far
        ]

    def send(slot, chip_step, there_core, kind, staged=False):
        source, buf, left, landed = kinds[kind]
        index = chip_step * pair + there_core
        if staged:
            origin = first.at[kind, index]
        else:
            origin = source.at[:, columns(there_core, head_of(slot, chip_at(chip_step)))]
        return pltpu.make_async_remote_copy(
            src_ref=origin, dst_ref=buf.at[slot, block_at(place), :],
            send_sem=left.at[slot, index], recv_sem=landed.at[slot, place],
            device_id={"seq": seq_of(chip_step, there_core), "mp": mp_index}, device_id_type=MESH,
        )

    def far_sends(slot, staged=False):
        return [send(slot, a, b, kind, staged) for kind in far_kinds(slot) for a, b in far]

    def near_sends(slot):
        return [
            send(slot, 0, lax.rem(core + step, pair), kind)
            for kind in range(3) for step in range(1, pair)
        ]

    def result(turn, slot, chip_step, core_step, mp_step):
        there_core = lax.rem(core + core_step, pair)
        there_mp = lax.rem(mp_index + mp_step, mp)
        source = o_buf.at[turn, pl.ds(pl.multiple_of(there_core * rows + there_mp * part, part), part), :]
        column = (mp_index * heads + core * per_core + head_of(slot, chip)) * HD
        target = out.at[:, pl.ds(pl.multiple_of(column, HD), HD)]
        index = core_step * mp + mp_step
        if chip_step == 0 and index == 0:
            return pltpu.make_async_copy(source, target, o_in.at[turn, index])
        return pltpu.make_async_remote_copy(
            src_ref=source, dst_ref=target, send_sem=o_out.at[turn, index], recv_sem=o_in.at[turn, index],
            device_id={"seq": seq_of(chip_step, there_core), "mp": there_mp}, device_id_type=MESH,
        )

    for copy in first_copies():
        copy.start()

    barrier = pltpu.get_barrier_semaphore()
    beside = [(seq_of(0, b), lax.rem(mp_index + m, mp)) for b in range(pair) for m in range(1, mp)]
    greeted = [(seq_of(a, b), mp_index) for a, b in far]
    greeted += [(seq_of(0, lax.rem(core + b, pair)), mp_index) for b in range(1, pair)]
    greeted += beside
    for there_seq, there_mp in greeted:
        pl.semaphore_signal(
            barrier, inc=1, device_id={"seq": there_seq, "mp": there_mp}, device_id_type=MESH
        )

    for copy in local_copies(0):
        copy.start()

    @pl.loop(1, held)
    def _(slot):
        for copy in local_copies(slot):
            copy.start()

    ends = []
    running = jnp.int32(0)
    for i in range(slots):
        running = running + lengths[bucket, i]
        ends.append(running)

    def ids(offset):
        found = jnp.zeros_like(offset)
        for end in ends:
            found = found + (offset >= end).astype(jnp.int32)
        return found

    k_ids = ids(lax.broadcasted_iota(jnp.int32, (1, group * rows), 1))

    for copy in first_copies():
        copy.wait()
    pl.semaphore_wait(barrier, len(greeted))

    for copy in far_sends(0, True) + near_sends(0):
        copy.start()

    @pl.loop(1, held)
    def _(slot):
        for copy in far_sends(slot) + near_sends(slot):
            copy.start()

    if extra:
        for there_seq, there_mp in beside:
            pl.semaphore_signal(
                ready, inc=1, device_id={"seq": there_seq, "mp": there_mp}, device_id_type=MESH
            )

    def arrived(kind, slot, base, count):
        buf, landed = kinds[kind][1], kinds[kind][3]
        for i in range(count):
            ref = buf.at[slot, block_at(base + i), :]
            pltpu.make_async_copy(ref, ref, landed.at[slot, base + i]).wait()

    factor = LOG2E / HD**0.5

    def weigh(slot, chip_step):
        keys = k_buf[slot]
        for b in range(pair):
            block = pl.ds(b * rows, rows)
            from_row = (chip_at(chip_step) * pair + b) * rows
            q_ids = ids(lax.broadcasted_iota(jnp.int32, (rows, 1), 0) + from_row)
            score = lax.dot_general(
                q_buf[slot, pl.ds(pl.multiple_of(from_row, rows), rows), :], keys,
                (((1,), (1,)), ((), ())), preferred_element_type=jnp.float32,
            )
            score = jnp.where(q_ids == k_ids, score, NEG)
            top = jnp.max(score, axis=1, keepdims=True)
            weight = jnp.exp2((score - top) * factor)
            t_buf[block, :] = jnp.broadcast_to(jnp.sum(weight, axis=1, keepdims=True), (rows, HD))
            p_buf[block, :] = weight.astype(jnp.bfloat16)

    def attend(turn, slot, chip_step):
        for core_step in reversed(range(pair)):
            block = block_at(lax.rem(core + core_step, pair))
            summed = jnp.dot(p_buf[block, :], v_buf[slot], preferred_element_type=jnp.float32)
            o_buf[turn, block, :] = (summed / t_buf[block, :]).astype(jnp.bfloat16)
            if chip_step == 0:
                for mp_step in reversed(range(mp)):
                    result(turn, slot, 0, core_step, mp_step).start()

    def far_results(mp_steps):
        return [
            result(a - 1, 0, a, core_step, mp_step)
            for mp_step in mp_steps for core_step in range(pair) for a in range(1, extra + 1)
        ]

    def settle(turn, slot, chip_step=0):
        for core_step in range(pair):
            for mp_step in range(mp):
                copy = result(turn, slot, chip_step, core_step, mp_step)
                if chip_step == 0 and core_step == 0 and mp_step == 0:
                    copy.wait()
                else:
                    copy.wait_send()
                    copy.wait_recv()

    begin = 0
    if extra:
        begin = 1
        arrived(0, 0, 0, group)
        arrived(1, 0, 0, group)
        for step in range(1, extra + 1):
            weigh(0, step)
            if step == 1:
                arrived(2, 0, 0, group)
            attend(step - 1, 0, step)
        weigh(0, 0)
        attend(extra, 0, 0)
        for copy in far_sends(0, True) + near_sends(0):
            copy.wait_send()

    @pl.loop(begin, held)
    def _(slot):
        arrived(0, slot, chip * pair, pair)
        arrived(1, slot, 0, group)
        if extra:
            @pl.when(slot == held - 1)
            def _():
                pl.semaphore_wait(ready, len(beside))
                for copy in far_results(list(range(1, mp)) + [0]):
                    copy.start()
        weigh(slot, 0)
        arrived(2, slot, 0, group)
        attend(slot + extra, slot, 0)
        for copy in far_sends(slot) + near_sends(slot):
            copy.wait_send()

        @pl.when(slot > begin)
        def _():
            settle(slot + extra - 1, slot - 1)

    if extra:
        settle(extra, 0)
    settle(held - 1 + extra, held - 1)
    for step in range(1, extra + 1):
        settle(step - 1, 0, step)


def shards(query, key, value, clip_lengths):
    rows, width = query.shape
    heads = width // HD
    group = lax.axis_size("seq") // clip_lengths.shape[0]
    mp = lax.axis_size("mp")
    pair = 2 if group % 2 == 0 and heads % 2 == 0 else 1
    per_core = heads // pair
    others = group // pair
    extra = others - 1 if per_core > others else 0
    held = per_core - extra
    dma = pltpu.SemaphoreType.DMA
    whole = pl.BlockSpec(memory_space=pl.ANY)
    return pl.pallas_call(
        functools.partial(kernel, group, pair, mp, heads, extra),
        out_shape=pltpu.VMEM((rows // mp, width * mp), jnp.bfloat16),
        in_specs=[pl.BlockSpec(memory_space=pltpu.SMEM), whole, whole, whole],
        out_specs=pl.BlockSpec(memory_space=pltpu.VMEM),
        scratch_shapes=[
            pltpu.VMEM((held, group * rows, HD), jnp.bfloat16),
            pltpu.VMEM((held, group * rows, HD), jnp.bfloat16),
            pltpu.VMEM((held, group * rows, HD), jnp.bfloat16),
            pltpu.VMEM((per_core, pair * rows, HD), jnp.bfloat16),
            pltpu.VMEM((3, group, rows, HD), jnp.bfloat16),
            pltpu.VMEM((pair * rows, group * rows), jnp.bfloat16),
            pltpu.VMEM((pair * rows, HD), jnp.float32),
            dma((held, group)), dma((held, group)), dma((held, group)), dma((per_core, pair * mp)),
            dma((held, group)), dma((held, group)), dma((held, group)), dma((per_core, pair * mp)),
            dma((3, group)), pltpu.SemaphoreType.REGULAR,
        ],
        compiler_params=pltpu.CompilerParams(collective_id=0, has_side_effects=True),
        name="packed_attention",
    )(clip_lengths, query, key, value)


def solution(mesh):
    in_specs = (P("seq", "mp"), P("seq", "mp"), P("seq", "mp"), P())
    out_specs = P(("seq", "mp"), None)
    return jax.shard_map(shards, mesh=mesh, in_specs=in_specs, out_specs=out_specs, check_vma=False)
```

time: 45.5 us -> 44.2 us (0.971)
  Pallas kernels: 44.4 us -> 43.1 us
    pallas_call x1, Pallas kernels: 44.4 us -> 43.1 us  [shards(): pl.pallas_call(functools.partial(kernel, group, pair, mp, heads, extra),...]
where the time goes in v3:
time: 44.2 us; the launch traced here: 44 us
  Pallas kernels  43.1 us (98%)
  local copies, waits for them, and re-layouts  0.88 us (2%)
    pallas_call x1, Pallas kernels, shards(): pl.pallas_call(functools.partial(kernel, group, pair, mp, heads, extra),...  43.1 us

profile of v3, /device:TPU:0, one launch (start us, length us, event | category | flops | bytes accessed | tf_op | source)
XLA Modules:
  0.0 44.0 jit_solution(5434905188601315162)
XLA Ops:
  0.0 43.1 %packed_attention.1 = bf16[128,3072]{1,0:T(8,128)(2,1)S(1)} custom-call(s32[4,4]{1,0:T(4,128)} %lengths.1, bf16[256,1536]{1,0:T(8,128)(2,1)} %query.1, bf16[256,1536]{1,0:T(8,128)(2,1)} %key.1, bf16[256,1536]{1,0:T(8,128)(2,1)} %value.1), custom_call_target="tpu_custom_call" | custom-call | tf_op jit(solution)/shard_map/packed_attention/pallas_call | solution.py:269
  43.1 0.9 %copy.6 = bf16[128,3072]{1,0:T(8,128)(2,1)} copy(bf16[128,3072]{1,0:T(8,128)(2,1)S(1)} %packed_attention.1) | data formatting | bytes 1572864

commit v4 on v3

--- a/solution.py
+++ b/solution.py
@@ -14,7 +14,7 @@
 
 
 def kernel(
-    group, pair, mp, heads, extra,
+    group, pair, mp, heads, lead,
     lengths, query, key, value, out,
     q_buf, k_buf, v_buf, o_buf, first, p_buf, t_buf,
     q_in, k_in, v_in, o_in, q_out, k_out, v_out, o_out, first_in, ready,
@@ -23,6 +23,7 @@
     part = rows // mp
     per_core = heads // pair
     others = group // pair
+    extra = lead * (others - 1)
     held = per_core - extra
     slots = lengths.shape[1]
     seq_index = lax.axis_index("seq")
@@ -39,8 +40,8 @@
         return bucket * group + chip_at(chip_step) * pair + there_core
 
     def head_of(slot, there_chip):
-        if extra and isinstance(slot, int) and slot == 0:
-            return there_chip
+        if isinstance(slot, int) and slot < lead:
+            return slot * others + there_chip
         return slot + extra
 
     def columns(owner, head):
@@ -59,7 +60,7 @@
         ]
 
     def far_kinds(slot):
-        whole = extra and isinstance(slot, int) and slot == 0
+        whole = isinstance(slot, int) and slot < lead
         return (0, 1, 2) if whole else (1, 2)
 
     far = [(chip_step, there_core) for there_core in range(pair) for chip_step in range(1, others)]
@@ -123,10 +124,11 @@
             barrier, inc=1, device_id={"seq": there_seq, "mp": there_mp}, device_id_type=MESH
         )
 
-    for copy in local_copies(0):
-        copy.start()
-
-    @pl.loop(1, held)
+    for slot in range(max(lead, 1)):
+        for copy in local_copies(slot):
+            copy.start()
+
+    @pl.loop(max(lead, 1), held)
     def _(slot):
         for copy in local_copies(slot):
             copy.start()
@@ -149,15 +151,16 @@
         copy.wait()
     pl.semaphore_wait(barrier, len(greeted))
 
-    for copy in far_sends(0, True) + near_sends(0):
-        copy.start()
-
-    @pl.loop(1, held)
+    for slot in range(max(lead, 1)):
+        for copy in far_sends(slot, slot == 0) + near_sends(slot):
+            copy.start()
+
+    @pl.loop(max(lead, 1), held)
     def _(slot):
         for copy in far_sends(slot) + near_sends(slot):
             copy.start()
 
-    if extra:
+    if lead:
         for there_seq, there_mp in beside:
             pl.semaphore_signal(
                 ready, inc=1, device_id={"seq": there_seq, "mp": there_mp}, device_id_type=MESH
@@ -198,8 +201,9 @@
 
     def far_results(mp_steps):
         return [
-            result(a - 1, 0, a, core_step, mp_step)
-            for mp_step in mp_steps for core_step in range(pair) for a in range(1, extra + 1)
+            result(slot * (others - 1) + a - 1, slot, a, core_step, mp_step)
+            for slot in range(lead) for mp_step in mp_steps
+            for core_step in range(pair) for a in range(1, others)
         ]
 
     def settle(turn, slot, chip_step=0):
@@ -212,46 +216,43 @@
                     copy.wait_send()
                     copy.wait_recv()
 
-    begin = 0
-    if extra:
-        begin = 1
-        arrived(0, 0, 0, group)
-        arrived(1, 0, 0, group)
-        for step in range(1, extra + 1):
-            weigh(0, step)
+    for slot in range(lead):
+        arrived(0, slot, 0, group)
+        arrived(1, slot, 0, group)
+        for step in range(1, others):
+            weigh(slot, step)
             if step == 1:
-                arrived(2, 0, 0, group)
-            attend(step - 1, 0, step)
-        weigh(0, 0)
-        attend(extra, 0, 0)
-        for copy in far_sends(0, True) + near_sends(0):
+                arrived(2, slot, 0, group)
+            attend(slot * (others - 1) + step - 1, slot, step)
+        weigh(slot, 0)
+        attend(slot + extra, slot, 0)
+        for copy in far_sends(slot, slot == 0) + near_sends(slot):
             copy.wait_send()
-
-    @pl.loop(begin, held)
+    if lead:
+        pl.semaphore_wait(ready, len(beside))
+        for copy in far_results(list(range(1, mp)) + [0]):
+            copy.start()
+
+    @pl.loop(lead, held)
     def _(slot):
         arrived(0, slot, chip * pair, pair)
         arrived(1, slot, 0, group)
-        if extra:
-            @pl.when(slot == held - 1)
-            def _():
-                pl.semaphore_wait(ready, len(beside))
-                for copy in far_results(list(range(1, mp)) + [0]):
-                    copy.start()
         weigh(slot, 0)
         arrived(2, slot, 0, group)
         attend(slot + extra, slot, 0)
         for copy in far_sends(slot) + near_sends(slot):
             copy.wait_send()
 
-        @pl.when(slot > begin)
+        @pl.when(slot > lead)
         def _():
             settle(slot + extra - 1, slot - 1)
 
-    if extra:
-        settle(extra, 0)
+    for slot in range(lead):
+        settle(slot + extra, slot)
     settle(held - 1 + extra, held - 1)
-    for step in range(1, extra + 1):
-        settle(step - 1, 0, step)
+    for slot in range(lead):
+        for step in range(1, others):
+            settle(slot * (others - 1) + step - 1, slot, step)
 
 
 def shards(query, key, value, clip_lengths):
@@ -262,12 +263,12 @@
     pair = 2 if group % 2 == 0 and heads % 2 == 0 else 1
     per_core = heads // pair
     others = group // pair
-    extra = others - 1 if per_core > others else 0
-    held = per_core - extra
+    lead = min(2, (per_core - 1) // others) if others > 1 else 0
+    held = per_core - lead * (others - 1)
     dma = pltpu.SemaphoreType.DMA
     whole = pl.BlockSpec(memory_space=pl.ANY)
     return pl.pallas_call(
-        functools.partial(kernel, group, pair, mp, heads, extra),
+        functools.partial(kernel, group, pair, mp, heads, lead),
         out_shape=pltpu.VMEM((rows // mp, width * mp), jnp.bfloat16),
         in_specs=[pl.BlockSpec(memory_space=pltpu.SMEM), whole, whole, whole],
         out_specs=pl.BlockSpec(memory_space=pltpu.VMEM),

time: 44.2 us -> 42.6 us (0.964)
  Pallas kernels: 43.1 us -> 41.5 us
    pallas_call x1, Pallas kernels: 43.1 us -> 41.5 us  [shards(): pl.pallas_call(functools.partial(kernel, group, pair, mp, heads, lead), o...]
where the time goes in v4:
time: 42.6 us; the launch traced here: 42.4 us
  Pallas kernels  41.5 us (97%)
  local copies, waits for them, and re-layouts  0.88 us (2%)
    pallas_call x1, Pallas kernels, shards(): pl.pallas_call(functools.partial(kernel, group, pair, mp, heads, lead), o...  41.5 us
    unnamed x1, local copies, waits for them, and re-layouts  0.88 us

profile of v4, /device:TPU:0, one launch (start us, length us, event | category | flops | bytes accessed | tf_op | source)
XLA Modules:
  0.0 42.4 jit_solution(7805610679569305266)
XLA Ops:
  0.0 41.5 %packed_attention.1 = bf16[128,3072]{1,0:T(8,128)(2,1)S(1)} custom-call(s32[4,4]{1,0:T(4,128)} %lengths.1, bf16[256,1536]{1,0:T(8,128)(2,1)} %query.1, bf16[256,1536]{1,0:T(8,128)(2,1)} %key.1, bf16[256,1536]{1,0:T(8,128)(2,1)} %value.1), custom_call_target="tpu_custom_call" | custom-call | tf_op jit(solution)/shard_map/packed_attention/pallas_call | solution.py:270
  41.6 0.9 %copy.6 = bf16[128,3072]{1,0:T(8,128)(2,1)} copy(bf16[128,3072]{1,0:T(8,128)(2,1)S(1)} %packed_attention.1) | data formatting | bytes 1572864
